TPU v7x, 128 devices: a whole 4x4x4 slice. The times are simulated.
128 devices in a mesh: jown: 8 (over y, core), pown: 16 (over x, z).
Axes of the slice: x: 4, y: 4, z: 4, core: 2. Of those that a mesh axis runs over, the one named last changes fastest.
Arguments:
- vertex: bfloat16 [128, 1024, 1024], P(('jown', 'pown')), may hold values from -6 to 6
- bare: bfloat16 [128, 1024, 1024], P(('jown', 'pown')), may hold values from -0.1875 to 0.1875
- pp_prop: float32 [128, 1024], P(('jown', 'pown')), may hold values from 0.3 to 3
- ph_prop: float32 [128, 1024], P(('jown', 'pown')), may hold values from 0.3 to 3
- orders: int32 [128], replicated, may hold values from 512 to 1024, as said below
- pandya_src: int32 [128, 4], replicated, may hold values from 0 to 127
- pandya_sixj: float32 [128, 4, 1024], P(None, None, ('jown', 'pown')), may hold values from -1 to 1
- back_src: int32 [128, 4], replicated, may hold values from 0 to 127
- back_sixj: float32 [128, 4, 1024], P(None, None, ('jown', 'pown')), may hold values from -1 to 1
Outputs:
- updated: bfloat16 [128, 1024, 1024], P(('jown', 'pown'))
Inputs may be any that keep to these rules, and one draw needn't show every extreme that they name: `orders`: some block has order exactly 1024.
All inputs are finite; a program needn't handle non-finite values.
Results may differ from a plain program's by a relative error of at most 0.0055.
Values may be sent and summed in bfloat16 or wider, within the bound.
A program may use at most 64 MiB of HBM per device.

v0:
```python
import math

import jax
import jax.numpy as jnp
from jax import lax
from jax.sharding import PartitionSpec as P


def cut_along(shard, dim, length):
    before, after = (shard.shape[:dim], shard.shape[dim + 1 :])
    return jnp.moveaxis(shard.reshape(*before, length, -1, *after), dim, 0)


def in_order(parts, dim):
    parts = jnp.moveaxis(parts, 0, dim)
    dims = parts.shape
    return parts.reshape(*dims[:dim], dims[dim] * dims[dim + 1], *dims[dim + 2 :])


def exchange_both(shard, axis, axes, splits, concats):
    sizes = [lax.axis_size(a) for a in axes]
    parts = cut_along(shard, splits[0], sizes[0])
    parts = jnp.moveaxis(cut_along(parts, splits[1] + 1, sizes[1]), 0, 1)
    inside = parts.shape[2:]
    parts = parts.reshape(-1, *inside)
    parts = lax.all_to_all(parts, axis, split_axis=0, concat_axis=0, tiled=True)
    parts = in_order(parts.reshape(*sizes, *inside), concats[0] + 1)
    return in_order(parts, concats[1])


def recouple(blocks, sources, factors, orders):
    jown_count = lax.axis_size("jown")
    pown_count = lax.axis_size("pown")
    per_owner = blocks.shape[0]
    total = per_owner * jown_count * pown_count
    width = blocks.shape[2]
    positions = jnp.arange(total, dtype=jnp.int32)
    tiles = exchange_both(blocks, ("jown", "pown"), ("jown", "pown"), (1, 1), (0, 0))
    pown_part = positions // (jown_count * per_owner)
    jown_part = positions // per_owner % jown_count
    owner_of = (jown_part * pown_count + pown_part) * per_owner + positions % per_owner
    tile_rows = tiles.shape[1]
    block_ids = sources[owner_of]
    jown_id = block_ids // (pown_count * per_owner)
    pown_id = block_ids // per_owner % pown_count
    picks = (pown_id * jown_count + jown_id) * per_owner + block_ids % per_owner
    weights = factors[owner_of]
    live_orders = orders[owner_of]
    summed = jnp.zeros((total, tile_rows, width), jnp.float32)
    for term in range(picks.shape[1]):
        summed = summed + weights[:, term, :, None] * tiles[picks[:, term]].astype(jnp.float32)
    row_ids = lax.axis_index(("jown", "pown")) * tile_rows + jnp.arange(tile_rows, dtype=jnp.int32)
    col_ids = jnp.arange(width, dtype=jnp.int32)
    keep = (row_ids[None, :, None] < live_orders[:, None, None]) & (
        col_ids[None, None, :] < live_orders[:, None, None]
    )
    mixed = jnp.where(keep, summed, 0.0).astype(jnp.bfloat16)
    return exchange_both(mixed, ("pown", "jown"), ("pown", "jown"), (0, 0), (1, 1))


def per_device(
    vertex, bare, pp_prop, ph_prop, orders, pandya_src, pandya_sixj, back_src, back_sixj
):
    per_owner = vertex.shape[0]
    width = vertex.shape[1]
    first = lax.axis_index(("jown", "pown")) * per_owner
    own_orders = lax.dynamic_slice_in_dim(orders, first, per_owner)
    live = (jnp.arange(width, dtype=jnp.int32)[None, :] < own_orders[:, None]).astype(jnp.float32)
    pair_live = live[:, :, None] * live[:, None, :]
    masked = (vertex.astype(jnp.float32) * pair_live).astype(jnp.bfloat16)
    scaled = (pp_prop[:, :, None] * masked.astype(jnp.float32)).astype(jnp.bfloat16)
    ladder = jnp.einsum("bij,bjk->bik", bare, scaled, preferred_element_type=jnp.float32)
    ph_blocks = recouple(masked, pandya_src, pandya_sixj, orders)
    weighted = (ph_blocks.astype(jnp.float32) * ph_prop[:, None, :]).astype(jnp.bfloat16)
    product = jnp.einsum("bij,bjk->bik", weighted, ph_blocks, preferred_element_type=jnp.float32)
    cycle = (product * (1.0 / math.sqrt(width))).astype(jnp.bfloat16)
    returned = recouple(cycle, back_src, back_sixj, orders)
    total = masked.astype(jnp.float32) + ladder + returned.astype(jnp.float32)
    return (total * pair_live).astype(jnp.bfloat16)


def solution(mesh):
    placed = (
        P(("jown", "pown"), None, None),
        P(("jown", "pown"), None, None),
        P(("jown", "pown"), None),
        P(("jown", "pown"), None),
        P(),
        P(),
        P(None, None, ("jown", "pown")),
        P(),
        P(None, None, ("jown", "pown")),
    )
    return jax.shard_map(
        per_device,
        mesh=mesh,
        in_specs=placed,
        out_specs=P(("jown", "pown"), None, None),
        check_vma=False,
    )
```

profile of v0, /device:TPU:1, one launch (start us, length us, event | category | flops | bytes accessed | tf_op | source)
XLA Modules:
  0.0 228.4 jit_solution(4570721930106330463)
XLA Ops:
  0.0 1.4 dynamic_slice.3
  1.4 0.6 fusion.49
  2.0 3.9 %copy.60 = bf16[1,1024,1024]{1,2,0:T(8,128)(2,1)} copy(bf16[1,1024,1024]{2,1,0:T(8,128)(2,1)} %param.9) | data formatting | bytes 4194304 | tf_op args[0]
  6.0 3.4 %fusion.4 = bf16[1,1024,1024]{1,2,0:T(8,128)(2,1)} fusion(bf16[1,1024,1024]{1,2,0:T(8,128)(2,1)} %copy.60, f32[1024]{0:T(1024)S(1)} %fusion.49), kind=kLoop, calls=%fused_computation.23 | loop fusion | flops 4194304 | bytes 4198400 | tf_op jit(solution)/shard_map/convert_element_type | solution.py:70
  9.4 4.0 %copy.63 = bf16[1,1024,1024]{2,1,0:T(8,128)(2,1)} copy(bf16[1,1024,1024]{1,2,0:T(8,128)(2,1)} %fusion.4) | data formatting | bytes 4194304 | tf_op jit(solution)/shard_map/convert_element_type | solution.py:70
  13.4 11.9 %all-to-all-start = ((bf16[128,1,8,1024]{3,2,1,0:T(8,128)(2,1)}), bf16[128,1,8,1024]{3,2,1,0:T(8,128)(2,1)}, u32[]{:S(2)}, u32[]{:S(2)}) async-start(bf16[128,1,8,1024]{3,2,1,0:T(8,128)(2,1)} %bitcast.106), calls=%async_computation | async-start | bytes 4194304 | tf_op jit(solution)/shard_map/all_to_all | solution.py:26
  25.3 0.1 copy.66
  25.4 0.1 fusion.44
  25.6 1.2 gather_fusion
  26.8 0.6 gather_fusion.3
  27.5 0.1 copy.62
  27.6 0.8 gather_fusion.2
  28.5 0.2 fusion.32
  28.8 0.1 iota_compare_fusion
  29.0 0.2 fusion.52
  29.2 25.4 %all-to-all-done = bf16[128,1,8,1024]{3,2,1,0:T(8,128)(2,1)} async-done(((bf16[128,1,8,1024]{3,2,1,0:T(8,128)(2,1)}), bf16[128,1,8,1024]{3,2,1,0:T(8,128)(2,1)}, u32[]{:S(2)}, u32[]{:S(2)}) %all-to-all-start) | async-done | bytes 2097184 | tf_op jit(solution)/shard_map/all_to_all | solution.py:26
  54.6 3.2 %copy.65 = bf16[16,8,1,8,1024]{4,3,1,0,2:T(8,128)(2,1)} copy(bf16[16,8,1,8,1024]{4,3,0,1,2:T(8,128)(2,1)} %bitcast.11) | data formatting | bytes 4194304 | tf_op jit(solution)/shard_map/transpose | solution.py:15
  57.8 3.7 %gather_fusion.4 = bf16[128,8,1024]{2,1,0:T(8,128)(2,1)} fusion(bf16[128,8,1024]{2,1,0:T(8,128)(2,1)} %bitcast.94, s32[1024]{0:T(1024)S(1)} %get-tuple-element.24), kind=kCustom, calls=%fused_computation.4 | custom fusion | bytes 4194816 | tf_op jit(solution)/shard_map/gather | solution.py:51
  61.4 3.6 %gather_fusion.5 = bf16[128,8,1024]{2,1,0:T(8,128)(2,1)} fusion(bf16[128,8,1024]{2,1,0:T(8,128)(2,1)} %bitcast.95, s32[1024]{0:T(1024)S(1)} %get-tuple-element.23), kind=kCustom, calls=%fused_computation.5 | custom fusion | bytes 4194816 | tf_op jit(solution)/shard_map/gather | solution.py:51
  65.1 3.6 %gather_fusion.6 = bf16[128,8,1024]{2,1,0:T(8,128)(2,1)} fusion(bf16[128,8,1024]{2,1,0:T(8,128)(2,1)} %bitcast.96, s32[1024]{0:T(1024)S(1)} %get-tuple-element.22), kind=kCustom, calls=%fused_computation.6 | custom fusion | bytes 4194816 | tf_op jit(solution)/shard_map/gather | solution.py:51
  68.7 3.6 %gather_fusion.7 = bf16[128,8,1024]{2,1,0:T(8,128)(2,1)} fusion(bf16[128,8,1024]{2,1,0:T(8,128)(2,1)} %bitcast.97, s32[1024]{0:T(1024)S(1)} %get-tuple-element.21), kind=kCustom, calls=%fused_computation.7 | custom fusion | bytes 4194816 | tf_op jit(solution)/shard_map/gather | solution.py:51
  72.2 4.6 %fusion.17 = bf16[128,1,8,1024]{3,2,1,0:T(8,128)(2,1)S(1)} fusion(bf16[128,8,1024]{2,1,0:T(8,128)(2,1)} %gather_fusion.7, f32[128,8]{1,0:T(8,128)S(1)} %bitcast.116, bf16[128,8,1024]{2,1,0:T(8,128)(2,1)} %gather_fusion.6, f32[128,8]{1,0:T(8,128)S(1)} %bitcast.114, bf16[128,8,1024]{2,1,0:T(8,128)(2,1)} %gather_fusion.5, f32[128,8]{1,0:T(8,128)S(1)} %bitcast.115, ...), kind=kLoop, calls=%fused_computation.46 | loop fusion | flops 14680064 | bytes 10634240 | tf_op jit(solution)/shard_map/convert_element_type | solution.py:57
  76.8 34.7 %all_to_all.20 = bf16[128,1,8,1024]{3,2,1,0:T(8,128)(2,1)S(1)} all-to-all(bf16[128,1,8,1024]{3,2,1,0:T(8,128)(2,1)S(1)} %fusion.17), channel_id=1, replica_groups=mesh['jown'=8,'pown'=16] {'pown','jown'}, dimensions={0} | all-to-all | bytes 4194304 | tf_op jit(solution)/shard_map/all_to_all | solution.py:26
  111.5 0.2 copy.69
  111.7 0.4 copy-done.4
  112.2 0.6 multiply_convert_fusion.1
  112.8 0.2 copy.68
  113.0 3.7 %fusion.18 = bf16[128,1,8,1024]{3,2,1,0:T(8,128)(2,1)} fusion(bf16[1024,1024]{1,0:T(8,128)(2,1)S(1)} %bitcast.108, bf16[1024,1024]{1,0:T(8,128)(2,1)S(1)} %bitcast.107), kind=kOutput, calls=%fused_computation.47 | convolution fusion | flops 2149580800 | bytes 6291456 | tf_op jit(solution)/shard_map/bij,bjk->bik/dot_general | solution.py:75
  116.7 5.9 %all-to-all-start.2 = ((bf16[128,1,8,1024]{3,2,1,0:T(8,128)(2,1)}), bf16[128,1,8,1024]{3,2,1,0:T(8,128)(2,1)}, u32[]{:S(2)}, u32[]{:S(2)}) async-start(bf16[128,1,8,1024]{3,2,1,0:T(8,128)(2,1)} %fusion.18), calls=%async_computation.2 | async-start | bytes 4194304 | tf_op jit(solution)/shard_map/all_to_all | solution.py:26
  122.6 0.1 copy.72
  122.7 0.6 gather_fusion.8
  123.4 0.1 copy.61
  123.5 0.8 gather_fusion.1
  124.4 0.2 fusion.36
  124.6 0.2 fusion.51
  124.8 27.2 %all-to-all-done.2 = bf16[128,1,8,1024]{3,2,1,0:T(8,128)(2,1)} async-done(((bf16[128,1,8,1024]{3,2,1,0:T(8,128)(2,1)}), bf16[128,1,8,1024]{3,2,1,0:T(8,128)(2,1)}, u32[]{:S(2)}, u32[]{:S(2)}) %all-to-all-start.2) | async-done | bytes 2097184 | tf_op jit(solution)/shard_map/all_to_all | solution.py:26
  152.0 3.2 %copy.71 = bf16[16,8,1,8,1024]{4,3,1,0,2:T(8,128)(2,1)} copy(bf16[16,8,1,8,1024]{4,3,0,1,2:T(8,128)(2,1)} %bitcast.30) | data formatting | bytes 4194304 | tf_op jit(solution)/shard_map/transpose | solution.py:15
  155.2 3.6 %gather_fusion.10 = bf16[128,8,1024]{2,1,0:T(8,128)(2,1)} fusion(bf16[128,8,1024]{2,1,0:T(8,128)(2,1)} %bitcast.98, s32[1024]{0:T(1024)S(1)} %get-tuple-element.27), kind=kCustom, calls=%fused_computation.10 | custom fusion | bytes 4194816 | tf_op jit(solution)/shard_map/gather | solution.py:51
  158.8 3.6 %gather_fusion.11 = bf16[128,8,1024]{2,1,0:T(8,128)(2,1)} fusion(bf16[128,8,1024]{2,1,0:T(8,128)(2,1)} %bitcast.99, s32[1024]{0:T(1024)S(1)} %get-tuple-element.26), kind=kCustom, calls=%fused_computation.11 | custom fusion | bytes 4194816 | tf_op jit(solution)/shard_map/gather | solution.py:51
  162.4 3.7 %gather_fusion.9 = bf16[128,8,1024]{2,1,0:T(8,128)(2,1)} fusion(bf16[128,8,1024]{2,1,0:T(8,128)(2,1)} %bitcast.100, s32[1024]{0:T(1024)S(1)} %get-tuple-element.28), kind=kCustom, calls=%fused_computation.9 | custom fusion | bytes 4194816 | tf_op jit(solution)/shard_map/gather | solution.py:51
  166.1 3.6 %gather_fusion.12 = bf16[128,8,1024]{2,1,0:T(8,128)(2,1)} fusion(bf16[128,8,1024]{2,1,0:T(8,128)(2,1)} %bitcast.101, s32[1024]{0:T(1024)S(1)} %get-tuple-element.25), kind=kCustom, calls=%fused_computation.12 | custom fusion | bytes 4194816 | tf_op jit(solution)/shard_map/gather | solution.py:51
  169.6 4.6 %fusion.16 = bf16[128,1,8,1024]{3,2,1,0:T(8,128)(2,1)S(1)} fusion(bf16[128,8,1024]{2,1,0:T(8,128)(2,1)} %gather_fusion.12, f32[128,8]{1,0:T(8,128)S(1)} %bitcast.112, bf16[128,8,1024]{2,1,0:T(8,128)(2,1)} %gather_fusion.11, f32[128,8]{1,0:T(8,128)S(1)} %bitcast.110, bf16[128,8,1024]{2,1,0:T(8,128)(2,1)} %gather_fusion.10, f32[128,8]{1,0:T(8,128)S(1)} %bitcast.111, ...), kind=kLoop, calls=%fused_computation.45 | loop fusion | flops 14680064 | bytes 10634240 | tf_op jit(solution)/shard_map/convert_element_type | solution.py:57
  174.2 34.7 %all_to_all.21 = bf16[128,1,8,1024]{3,2,1,0:T(8,128)(2,1)S(1)} all-to-all(bf16[128,1,8,1024]{3,2,1,0:T(8,128)(2,1)S(1)} %fusion.16), channel_id=1, replica_groups=mesh['jown'=8,'pown'=16] {'pown','jown'}, dimensions={0} | all-to-all | bytes 4194304 | tf_op jit(solution)/shard_map/all_to_all | solution.py:26
  208.9 0.5 convert_bitcast_fusion
  209.4 2.3 copy.75
  211.7 5.4 %copy.76 = f32[1,1024,1024]{1,2,0:T(8,128)} copy(f32[1,1024,1024]{2,1,0:T(8,128)} %bitcast.104) | data formatting | bytes 8388608 | tf_op jit(solution)/shard_map/convert_element_type | solution.py:78
  217.0 7.4 %fusion.5 = bf16[1,1024,1024]{1,2,0:T(8,128)(2,1)} fusion(f32[1,1024,1024]{1,2,0:T(8,128)} %copy.76, bf16[1,1024,1024]{2,1,0:T(8,128)(2,1)S(1)} %copy-done, f32[1024]{0:T(1024)S(1)} %bitcast.118, f32[1024]{0:T(1024)S(1)} %fusion.49, bf16[1,1024,1024]{1,2,0:T(8,128)(2,1)} %copy.60), kind=kOutput, calls=%fused_computation.24 | convolution fusion | flops 2164260864 | bytes 10493952 | tf_op jit(solution)/shard_map/bij,bjk->bik/dot_general | solution.py:72
  224.4 3.9 %copy.77 = bf16[1,1024,1024]{2,1,0:T(8,128)(2,1)} copy(bf16[1,1024,1024]{1,2,0:T(8,128)(2,1)} %fusion.5) | data formatting | bytes 4194304 | tf_op jit(solution)/shard_map/convert_element_type | solution.py:79
  (24 shorter events, 0.3 us)
Async XLA Ops:
  0.0 217.0 %copy-start = (bf16[1,1024,1024]{2,1,0:T(8,128)(2,1)S(1)}, bf16[1,1024,1024]{2,1,0:T(8,128)(2,1)}, u32[]{:S(2)}) copy-start(bf16[1,1024,1024]{2,1,0:T(8,128)(2,1)} %param.10) | copy-start | bytes 6291460
  13.4 12.0 %copy-start.5 = (s32[128,4]{0,1:T(4,128)S(1)}, s32[128,4]{0,1:T(4,128)}, u32[]{:S(2)}) copy-start(s32[128,4]{0,1:T(4,128)} %param.14) | copy-start | bytes 6148
  13.4 12.2 %copy-start.1 = (s32[128]{0:T(128)S(1)}, s32[128]{0:T(128)}, u32[]{:S(2)}) copy-start(s32[128]{0:T(128)} %param.13) | copy-start | bytes 1540
  13.4 14.1 %copy-start.2 = (f32[128,4,8]{0,2,1:T(8,128)S(1)}, f32[128,4,8]{0,2,1:T(8,128)}, u32[]{:S(2)}) copy-start(f32[128,4,8]{0,2,1:T(8,128)} %param.15) | copy-start | bytes 49156
  13.4 41.2 %all-to-all-start = ((bf16[128,1,8,1024]{3,2,1,0:T(8,128)(2,1)}), bf16[128,1,8,1024]{3,2,1,0:T(8,128)(2,1)}, u32[]{:S(2)}, u32[]{:S(2)}) async-start(bf16[128,1,8,1024]{3,2,1,0:T(8,128)(2,1)} %bitcast.106), calls=%async_computation | async-start | bytes 4194304 | tf_op jit(solution)/shard_map/all_to_all | solution.py:26
  111.5 0.7 copy-start.4
  116.7 5.9 %copy-start.6 = (s32[128,4]{0,1:T(4,128)S(1)}, s32[128,4]{0,1:T(4,128)}, u32[]{:S(2)}) copy-start(s32[128,4]{0,1:T(4,128)} %param.16) | copy-start | bytes 6148
  116.7 6.7 %copy-start.3 = (f32[128,4,8]{0,2,1:T(8,128)S(1)}, f32[128,4,8]{0,2,1:T(8,128)}, u32[]{:S(2)}) copy-start(f32[128,4,8]{0,2,1:T(8,128)} %param.17) | copy-start | bytes 49156
  116.7 35.3 %all-to-all-start.2 = ((bf16[128,1,8,1024]{3,2,1,0:T(8,128)(2,1)}), bf16[128,1,8,1024]{3,2,1,0:T(8,128)(2,1)}, u32[]{:S(2)}, u32[]{:S(2)}) async-start(bf16[128,1,8,1024]{3,2,1,0:T(8,128)(2,1)} %fusion.18), calls=%async_computation.2 | async-start | bytes 4194304 | tf_op jit(solution)/shard_map/all_to_all | solution.py:26
  211.7 5.4 %copy-start.7 = (f32[1,1024]{1,0:T(1,128)S(1)}, f32[1,1024]{1,0:T(1,128)}, u32[]{:S(2)}) copy-start(f32[1,1024]{1,0:T(1,128)} %param.11) | copy-start | bytes 12292
where the time goes:
time: 229 us; the launch traced here: 228 us
  blocking collectives  69.3 us (30%)
  local copies, waits for them, and re-layouts  61.9 us (27%)
  waiting for transfers between devices  52.6 us (23%)
  starting transfers between devices  17.8 us (8%)
  other arithmetic  15.3 us (7%)
  matrix products  11.1 us (5%)
    all_to_all x2, blocking collectives, exchange_both(): parts = lax.all_to_all(parts, axis, split_axis=0, concat_axis=0, tiled=True)  69.3 us
    all_to_all x2, waiting for transfers between devices, exchange_both(): parts = lax.all_to_all(parts, axis, split_axis=0, concat_axis=0, tiled=True)  52.6 us
    gather x8, local copies, waits for them, and re-layouts, recouple(): tiles[picks[:, term]].astype(jnp.float32)  28.9 us
    all_to_all x2, starting transfers between devices, exchange_both(): parts = lax.all_to_all(parts, axis, split_axis=0, concat_axis=0, tiled=True)  17.8 us
    convert_element_type x2, other arithmetic, recouple(): mixed = jnp.where(keep, summed, 0.0).astype(jnp.bfloat16)  9.15 us
    convert_element_type x2, local copies, waits for them, and re-layouts, per_device(): total = masked.astype(jnp.float32) + ladder + returned.astype(jnp.float32)  7.64 us
    dot_general x1, matrix products, per_device(): jnp.einsum('bij,bjk->bik', bare, scaled, preferred_element_type=jnp.float32)  7.41 us
    transpose x3, local copies, waits for them, and re-layouts, in_order(): parts = jnp.moveaxis(parts, 0, dim)  6.6 us
  transfers between devices with their start and end apart: 2, of which 2 were waited for; matrix products, arithmetic and copies ran while one was open for 3% of the time, Pallas kernels for 0%

commit v1 on v0

v1 whole, which is shorter than its diff:
```python
import functools
import math

import jax
import jax.numpy as jnp
from jax import lax
from jax.experimental import pallas as pl
from jax.experimental.pallas import tpu as pltpu
from jax.sharding import PartitionSpec as P

MESH = pl.DeviceIdType.MESH
F32, BF16 = jnp.float32, jnp.bfloat16
STRIDE = 37


def kernel(
    dims,
    orders_ref,
    psrc_ref,
    bsrc_ref,
    bands_ref,
    vertex_ref,
    bare_ref,
    pp_ref,
    php_ref,
    psix_ref,
    bsix_ref,
    out_ref,
    vbuf,
    bbuf,
    base,
    wide,
    recv_a,
    mix_a,
    ph_bands,
    ph,
    weighted,
    cyc,
    recv_b,
    mix_b,
    ret_bands,
    load_sem,
    send_sem,
    recv_sem,
):
    n_j, n_p, n_y, n_x, n_z, cores = dims
    total = n_j * n_p
    m = ph.shape[0]
    band = m // total
    tiles = m // 128
    me_j, me_p = lax.axis_index("jown"), lax.axis_index("pown")
    me = me_j * n_p + me_p
    my_y, my_c = me_j // cores, me_j % cores
    my_x, my_z = me_p // n_z, me_p % n_z

    def peer_of(step):
        o = (step * STRIDE) % total
        z = (my_z + o % n_z) % n_z
        o = o // n_z
        x = (my_x + o % n_x) % n_x
        o = o // n_x
        c = (my_c + o % cores) % cores
        o = o // cores
        y = (my_y + o) % n_y
        return y * cores + c, x * n_z + z

    def exchange(src, dst, phase):
        @pl.loop(1, total)
        def _(step):
            j, p = peer_of(step)
            pltpu.make_async_remote_copy(
                src_ref=src.at[j * n_p + p],
                dst_ref=dst.at[me],
                send_sem=send_sem.at[phase],
                recv_sem=recv_sem.at[phase],
                device_id=(j, p),
                device_id_type=MESH,
            ).start()

    def arrived(dst, phase):
        part = dst.at[pl.ds(0, total - 1)]
        pltpu.make_async_copy(part, part, recv_sem.at[phase]).wait()

    def sent(src, phase):
        part = src.at[pl.ds(0, total - 1)]
        pltpu.make_async_copy(part, part, send_sem.at[phase]).wait()

    own = pltpu.make_async_copy(bands_ref.at[me], recv_a.at[me], load_sem.at[0])
    own.start()
    load_v = pltpu.make_async_copy(vertex_ref, vbuf, load_sem.at[1])
    load_v.start()
    load_b = pltpu.make_async_copy(bare_ref, bbuf, load_sem.at[2])
    load_b.start()
    exchange(bands_ref, recv_a, 0)

    my_order = orders_ref[me]
    sub = lax.broadcasted_iota(jnp.int32, (8, 128), 0)
    lane = lax.broadcasted_iota(jnp.int32, (8, 128), 1)
    row_id = me * band + sub

    def spread(six_ref, slot):
        for k in range(4):
            six = six_ref[k]
            for c in range(total):
                wide[slot, c, k] = jnp.broadcast_to(six[:, c : c + 1], (8, 128))

    spread(psix_ref, 0)
    spread(bsix_ref, 1)

    load_v.wait()
    load_b.wait()
    col_live = (lax.broadcasted_iota(jnp.int32, (1, m), 1) < my_order).astype(F32)

    @pl.loop(0, m // 128)
    def _(i):
        rows = pl.ds(pl.multiple_of(i * 128, 128), 128)
        ids = i * 128 + lax.broadcasted_iota(jnp.int32, (128, 1), 0)
        row_live = (ids < my_order).astype(F32)
        masked = vbuf[rows, :].astype(F32) * col_live * row_live
        base[rows, :] = masked
        weighted[rows, :] = (masked * pp_ref[rows, :]).astype(BF16)

    @pl.loop(0, m // 128)
    def _(i):
        rows = pl.ds(pl.multiple_of(i * 128, 128), 128)
        base[rows, :] += jnp.dot(bbuf[rows, :], weighted[...], preferred_element_type=F32)

    def recouple(recv, mix, src_ref, slot, source_mask):
        @pl.loop(0, total)
        def _(c):
            order = orders_ref[c]
            acc = [jnp.zeros((8, 128), F32) for _ in range(tiles)]
            for k in range(4):
                s = src_ref[k, c]
                bound = order
                if source_mask:
                    bound = jnp.minimum(order, orders_ref[s])
                w = jnp.where(row_id < bound, wide[slot, c, k], 0.0)
                x = recv[s].astype(F32)
                for t in range(tiles):
                    term = w * x[8 * t : 8 * t + 8]
                    if source_mask:
                        term = jnp.where(lane + 128 * t < bound, term, 0.0)
                    acc[t] = acc[t] + term
            if not source_mask:
                acc = [jnp.where(lane + 128 * t < order, a, 0.0) for t, a in enumerate(acc)]
            mix[c] = jnp.concatenate(acc, axis=0).astype(BF16)

    arrived(recv_a, 0)
    own.wait()
    recouple(recv_a, mix_a, psrc_ref, 0, True)
    exchange(mix_a, ph_bands, 1)
    ph_bands[me] = mix_a[me]
    arrived(ph_bands, 1)

    @pl.loop(0, total // 2)
    def _(q):
        a = ph_bands[2 * q].astype(F32)
        b = ph_bands[2 * q + 1].astype(F32)
        rows = pl.ds(pl.multiple_of(q * 16, 16), 16)
        for t in range(tiles):
            cols = slice(128 * t, 128 * t + 128)
            tile = jnp.concatenate([a[8 * t : 8 * t + 8], b[8 * t : 8 * t + 8]], axis=0)
            ph[rows, cols] = tile.astype(BF16)
            weighted[rows, cols] = (tile * php_ref[:, cols]).astype(BF16)

    @pl.loop(0, m // 128)
    def _(i):
        rows = pl.ds(pl.multiple_of(i * 128, 128), 128)
        prod = jnp.dot(weighted[rows, :], ph[...], preferred_element_type=F32) * (1.0 / math.sqrt(m))
        for b in range(128 // band):
            parts = [prod[band * b : band * b + band, 128 * t : 128 * t + 128] for t in range(tiles)]
            cyc[i * (128 // band) + b] = jnp.concatenate(parts, axis=0).astype(BF16)

    exchange(cyc, recv_b, 2)
    recv_b[me] = cyc[me]
    arrived(recv_b, 2)
    recouple(recv_b, mix_b, bsrc_ref, 1, False)
    exchange(mix_b, ret_bands, 3)
    ret_bands[me] = mix_b[me]
    arrived(ret_bands, 3)

    @pl.loop(0, total // 2)
    def _(q):
        a = ret_bands[2 * q].astype(F32)
        b = ret_bands[2 * q + 1].astype(F32)
        rows = pl.ds(pl.multiple_of(q * 16, 16), 16)
        ids = q * 16 + lax.broadcasted_iota(jnp.int32, (16, 128), 0)
        for t in range(tiles):
            cols = slice(128 * t, 128 * t + 128)
            tile = jnp.concatenate([a[8 * t : 8 * t + 8], b[8 * t : 8 * t + 8]], axis=0)
            col_ids = 128 * t + lax.broadcasted_iota(jnp.int32, (16, 128), 1)
            keep = (ids < my_order) & (col_ids < my_order)
            out_ref[rows, cols] = jnp.where(keep, base[rows, cols] + tile, 0.0).astype(BF16)

    sent(recv_a, 0)
    sent(mix_a, 1)
    sent(cyc, 2)
    sent(mix_b, 3)


def per_device(dims, vertex, bare, pp_prop, ph_prop, orders, pandya_src, pandya_sixj, back_src, back_sixj):
    m = vertex.shape[1]
    n_j, n_p = dims[:2]
    total = n_j * n_p
    band = m // total
    tiles = m // 128
    flat = vertex.reshape(m, m)
    bands = flat.reshape(total, band, tiles, 128).transpose(0, 2, 1, 3).reshape(total, tiles * band, 128)
    tile_buf = pltpu.VMEM((total, tiles * band, 128), BF16)
    square = pltpu.VMEM((m, m), BF16)
    smem = pl.BlockSpec(memory_space=pltpu.SMEM)
    vmem = pl.BlockSpec(memory_space=pltpu.VMEM)
    hbm = pl.BlockSpec(memory_space=pl.ANY)
    out = pl.pallas_call(
        functools.partial(kernel, dims),
        out_shape=jax.ShapeDtypeStruct((m, m), BF16),
        in_specs=[smem] * 3 + [hbm] * 3 + [vmem] * 4,
        out_specs=vmem,
        scratch_shapes=[
            square,
            square,
            pltpu.VMEM((m, m), F32),
            pltpu.VMEM((2, total, 4, 8, 128), F32),
            tile_buf,
            tile_buf,
            tile_buf,
            square,
            square,
            tile_buf,
            tile_buf,
            tile_buf,
            tile_buf,
            pltpu.SemaphoreType.DMA((3,)),
            pltpu.SemaphoreType.DMA((4,)),
            pltpu.SemaphoreType.DMA((4,)),
        ],
        compiler_params=pltpu.CompilerParams(has_side_effects=True, vmem_limit_bytes=56 * 1024 * 1024),
        name="parquet",
    )(
        orders,
        pandya_src.T,
        back_src.T,
        bands,
        flat,
        bare.reshape(m, m),
        pp_prop.reshape(m, 1),
        ph_prop,
        pandya_sixj.transpose(1, 2, 0),
        back_sixj.transpose(1, 2, 0),
    )
    return out.reshape(1, m, m)


def solution(mesh):
    n_j, n_p = mesh.shape["jown"], mesh.shape["pown"]
    cores = 2
    side = math.isqrt(n_p)
    dims = (n_j, n_p, n_j // cores, side, n_p // side, cores)
    placed = (
        P(("jown", "pown"), None, None),
        P(("jown", "pown"), None, None),
        P(("jown", "pown"), None),
        P(("jown", "pown"), None),
        P(),
        P(),
        P(None, None, ("jown", "pown")),
        P(),
        P(None, None, ("jown", "pown")),
    )
    return jax.shard_map(
        functools.partial(per_device, dims),
        mesh=mesh,
        in_specs=placed,
        out_specs=P(("jown", "pown"), None, None),
        check_vma=False,
    )
```

time: 229 us -> 143 us (0.62)
  Pallas kernels: 0 us -> 138 us
  blocking collectives: 69.3 us -> 0 us
  local copies, waits for them, and re-layouts: 61.9 us -> 4.79 us
  waiting for transfers between devices: 52.6 us -> 0 us
  starting transfers between devices: 17.8 us -> 0 us
  other arithmetic: 15.3 us -> 0 us
  matrix products: 11.1 us -> 0 us
    pallas_call x0 -> x1, Pallas kernels: none -> 138 us  [per_device(): pl.pallas_call(functools.partial(kernel, dims), out_shape=jax.ShapeDtypeS...]
    all_to_all x2 -> x0, blocking collectives: 69.3 us -> none  [exchange_both(): parts = lax.all_to_all(parts, axis, split_axis=0, concat_axis=0, tiled=True)]
    all_to_all x2 -> x0, waiting for transfers between devices: 52.6 us -> none  [exchange_both(): parts = lax.all_to_all(parts, axis, split_axis=0, concat_axis=0, tiled=True)]
    gather x13 -> x0, local copies, waits for them, and re-layouts: 32.9 us -> none  [the longest x8 28.9 us: recouple(): tiles[picks[:, term]].astype(jnp.float32)]
    all_to_all x2 -> x0, starting transfers between devices: 17.8 us -> none  [exchange_both(): parts = lax.all_to_all(parts, axis, split_axis=0, concat_axis=0, tiled=True)]
    convert_element_type x5 -> x0, local copies, waits for them, and re-layouts: 15.8 us -> none  [the longest x2 7.64 us: per_device(): total = masked.astype(jnp.float32) + ladder + returned.astype(jnp.float32)]
    convert_element_type x6 -> x0, other arithmetic: 14.3 us -> none  [the longest x2 9.15 us: recouple(): mixed = jnp.where(keep, summed, 0.0).astype(jnp.bfloat16)]
    dot_general x2 -> x0, matrix products: 11.1 us -> none  [the longest x1 7.41 us: per_device(): jnp.einsum('bij,bjk->bik', bare, scaled, preferred_element_type=jnp.float32)]
  transfers between devices with their start and end apart: 2 -> 0, of which waited for: 2 -> 0; matrix products, arithmetic and copies ran while one was open for 3% -> 0% of each run, Pallas kernels for 0% -> 0%
where the time goes in v1:
time: 143 us
  Pallas kernels  138 us (97%)
  local copies, waits for them, and re-layouts  4.79 us (3%)
    pallas_call x1, Pallas kernels, per_device(): pl.pallas_call(functools.partial(kernel, dims), out_shape=jax.ShapeDtypeS...  138 us
    unnamed x1, local copies, waits for them, and re-layouts  3.08 us

profile of v1, /device:TPU:1, one launch (start us, length us, event | category | flops | bytes accessed | tf_op | source)
XLA Modules:
  0.0 142.9 jit_solution(16967527637446961813)
XLA Ops:
  0.0 1.7 %copy.10.pp_ref = f32[1024,1]{1,0:T(8,128)} copy(f32[1024,1]{0,1:T(1,128)} %bitcast.19) | data formatting | bytes 8192 | tf_op jit(solution)/shard_map/reshape | solution.py:247
  1.7 138.1 %parquet.1 = bf16[1024,1024]{1,0:T(8,128)(2,1)} custom-call(s32[128]{0:T(128)} %orders_ref.1, s32[4,128]{1,0:T(4,128)} %bitcast.20, s32[4,128]{1,0:T(4,128)} %bitcast.21, bf16[128,64,128]{2,1,0:T(8,128)(2,1)} %bitcast.14, bf16[1024,1024]{1,0:T(8,128)(2,1)} %bitcast.15, bf16[1024,1024]{1,0:T(8,128)(2,1)} %bitcast.16, f32[1024,1]{1,0:T(8,128)} %copy.10.pp_ref, ...), custom_call_target="tpu_custom_call" | custom-call | tf_op jit(solution)/shard_map/parquet/pallas_call | solution.py:215
  139.8 3.1 %copy.12 = bf16[1,1024,1024]{2,1,0:T(8,128)(2,1)} copy(bf16[1,1024,1024]{2,1,0:T(8,128)(2,1)} %bitcast.13) | data formatting | bytes 4194304

commit v2 on v1

v2 whole, which is shorter than its diff:
```python
import functools
import math

import jax
import jax.numpy as jnp
from jax import lax
from jax.experimental import pallas as pl
from jax.experimental.pallas import tpu as pltpu
from jax.sharding import PartitionSpec as P

MESH = pl.DeviceIdType.MESH
F32, BF16 = jnp.float32, jnp.bfloat16
STRIDE = 37
PARTS = 2
VMEM_MIB = 42


def kernel(
    dims,
    orders_hbm,
    psrc_hbm,
    bsrc_hbm,
    bands_hbm,
    vertex_hbm,
    bare_hbm,
    pp_hbm,
    php_hbm,
    psix_hbm,
    bsix_hbm,
    out_ref,
    orders_ref,
    psrc_ref,
    bsrc_ref,
    pp_ref,
    php_ref,
    psix_ref,
    bsix_ref,
    vbuf,
    bbuf,
    base,
    wide,
    mix_a,
    ph_bands,
    ph,
    weighted,
    cyc,
    mix_b,
    ret_bands,
    load_sem,
    send_sem,
    recv_sem,
    gate_sem,
    *recv,
):
    recv_a, recv_b = recv[:PARTS], recv[PARTS:]
    n_j, n_p, n_y, n_x, n_z, cores = dims
    total = n_j * n_p
    m = ph.shape[0]
    band = m // total
    tiles = m // 128 // PARTS
    me_j, me_p = lax.axis_index("jown"), lax.axis_index("pown")
    me = me_j * n_p + me_p
    my_y, my_c = me_j // cores, me_j % cores
    my_x, my_z = me_p // n_z, me_p % n_z

    def shifted(y, c, x, z):
        j = (my_y + y) % n_y * cores + (my_c + c) % cores
        return j, (my_x + x) % n_x * n_z + (my_z + z) % n_z

    def peer_of(step):
        o = (step * STRIDE) % total
        z = o % n_z
        o = o // n_z
        x = o % n_x
        o = o // n_x
        return shifted(o // cores, o % cores, x, z)

    def send(src, dst, phase, part, j, p):
        pltpu.make_async_remote_copy(
            src_ref=src,
            dst_ref=dst,
            send_sem=send_sem.at[phase],
            recv_sem=recv_sem.at[phase, part],
            device_id=(j, p),
            device_id_type=MESH,
        ).start()

    def arrived(phase, part):
        span = mix_a.at[0, pl.ds(0, total - 1)]
        pltpu.make_async_copy(span, span, recv_sem.at[phase, part]).wait()

    barrier = pltpu.get_barrier_semaphore()
    column = [(o // cores, o % cores, 0, 0) for o in range(1, n_j)]
    plane = [(0, 0, o // n_z, o % n_z) for o in range(1, n_p)]
    for offset in column + plane:
        pl.semaphore_signal(barrier, inc=1, device_id=shifted(*offset), device_id_type=MESH)

    def load(src, dst, slot):
        copy = pltpu.make_async_copy(src, dst, load_sem.at[slot])
        copy.start()
        return copy

    rows_of = [pl.ds(part * tiles * band, tiles * band) for part in range(PARTS)]
    own = [load(bands_hbm.at[me, rows_of[part]], recv_a[part].at[me], 9 + part) for part in range(PARTS)]
    loads = [
        load(src, dst, slot)
        for slot, (src, dst) in enumerate(
            (
                (orders_hbm, orders_ref),
                (psrc_hbm, psrc_ref),
                (bsrc_hbm, bsrc_ref),
                (pp_hbm, pp_ref),
                (php_hbm, php_ref),
                (psix_hbm, psix_ref),
                (bsix_hbm, bsix_ref),
                (vertex_hbm, vbuf),
                (bare_hbm, bbuf),
            )
        )
    ]
    pl.semaphore_wait(barrier, len(column) + len(plane))
    for offset in column:
        pl.semaphore_signal(gate_sem, inc=1, device_id=shifted(*offset), device_id_type=MESH)
    pl.semaphore_wait(gate_sem, len(column))

    for part in range(PARTS):

        @pl.loop(1, total)
        def _(step):
            j, p = peer_of(step)
            send(bands_hbm.at[j * n_p + p, rows_of[part]], recv_a[part].at[me], 0, part, j, p)

    for copy in loads:
        copy.wait()
    my_order = orders_ref[me]
    lane = lax.broadcasted_iota(jnp.int32, (8, 128), 1)
    row_id = me * band + lax.broadcasted_iota(jnp.int32, (8, 128), 0)

    def spread(six_ref, slot):
        for k in range(4):
            six = six_ref[k]
            for c in range(total):
                wide[slot, c, k] = jnp.broadcast_to(six[:, c : c + 1], (8, 128))

    spread(psix_ref, 0)

    col_live = (lax.broadcasted_iota(jnp.int32, (1, m), 1) < my_order).astype(F32)

    @pl.loop(0, m // 128)
    def _(i):
        rows = pl.ds(pl.multiple_of(i * 128, 128), 128)
        ids = i * 128 + lax.broadcasted_iota(jnp.int32, (128, 1), 0)
        row_live = (ids < my_order).astype(F32)
        scale = jnp.broadcast_to(pp_ref[:, rows], (128, 128)).T
        masked = vbuf[rows, :].astype(F32) * col_live * row_live
        base[rows, :] = masked
        for t in range(m // 128):
            cols = slice(128 * t, 128 * t + 128)
            weighted[rows, cols] = (masked[:, cols] * scale).astype(BF16)

    @pl.loop(0, m // 256)
    def _(i):
        rows = pl.ds(pl.multiple_of(i * 256, 256), 256)
        base[rows, :] += jnp.dot(bbuf[rows, :], weighted[...], preferred_element_type=F32)

    spread(bsix_ref, 1)

    def recouple(recv, part, mix, landing, src_ref, slot, source_mask, phase):
        first = 128 * tiles * part

        def mixed(c):
            order = orders_ref[c]
            acc = [jnp.zeros((8, 128), F32) for _ in range(tiles)]
            for k in range(4):
                s = src_ref[k, c]
                bound = order
                if source_mask:
                    bound = jnp.minimum(order, orders_ref[s])
                w = jnp.where(row_id < bound, wide[slot, c, k], 0.0)
                x = recv[s].astype(F32)
                for t in range(tiles):
                    term = w * x[8 * t : 8 * t + 8]
                    if source_mask:
                        term = jnp.where(lane + (first + 128 * t) < bound, term, 0.0)
                    acc[t] = acc[t] + term
            if not source_mask:
                acc = [jnp.where(lane + (first + 128 * t) < order, a, 0.0) for t, a in enumerate(acc)]
            return jnp.concatenate(acc, axis=0).astype(BF16)

        def store(step):
            j, p = peer_of(step)
            c = j * n_p + p
            mix[part, c] = mixed(c)

        def leave(step):
            j, p = peer_of(step)
            send(mix.at[part, j * n_p + p], landing.at[part, me], phase, part, j, p)

        store(1)

        @pl.loop(2, total)
        def _(step):
            store(step)
            leave(step - 1)

        landing[part, me] = mixed(me)
        leave(total - 1)

    for part in range(PARTS):
        own[part].wait()
        arrived(0, part)
        recouple(recv_a[part], part, mix_a, ph_bands, psrc_ref, 0, True, 1)

    def pair(bands, part, q):
        a = bands[part, 2 * q].astype(F32)
        b = bands[part, 2 * q + 1].astype(F32)
        return [
            jnp.concatenate([a[8 * t : 8 * t + 8], b[8 * t : 8 * t + 8]], axis=0) for t in range(tiles)
        ]

    for part in range(PARTS):
        arrived(1, part)

        @pl.loop(0, total // 2)
        def _(q):
            rows = pl.ds(pl.multiple_of(q * 16, 16), 16)
            for t, tile in enumerate(pair(ph_bands, part, q)):
                first = 128 * (part * tiles + t)
                cols = slice(first, first + 128)
                ph[rows, cols] = tile.astype(BF16)
                weighted[rows, cols] = (tile * php_ref[:, cols]).astype(BF16)

    for part in range(PARTS):
        cols = slice(128 * tiles * part, 128 * tiles * (part + 1))

        @pl.loop(0, m // 256)
        def _(i):
            rows = pl.ds(pl.multiple_of(i * 256, 256), 256)
            prod = jnp.dot(weighted[rows, :], ph[:, cols], preferred_element_type=F32)
            prod = prod * (1.0 / math.sqrt(m))
            for b in range(256 // band):
                lines = [prod[band * b : band * b + band, 128 * t : 128 * t + 128] for t in range(tiles)]
                cyc[part, i * (256 // band) + b] = jnp.concatenate(lines, axis=0).astype(BF16)

        @pl.loop(1, total)
        def _(step):
            j, p = peer_of(step)
            send(cyc.at[part, j * n_p + p], recv_b[part].at[me], 2, part, j, p)

        recv_b[part][me] = cyc[part, me]

    for part in range(PARTS):
        arrived(2, part)
        recouple(recv_b[part], part, mix_b, ret_bands, bsrc_ref, 1, False, 3)

    for part in range(PARTS):
        arrived(3, part)

        @pl.loop(0, total // 2)
        def _(q):
            rows = pl.ds(pl.multiple_of(q * 16, 16), 16)
            ids = q * 16 + lax.broadcasted_iota(jnp.int32, (16, 128), 0)
            for t, tile in enumerate(pair(ret_bands, part, q)):
                first = 128 * (part * tiles + t)
                cols = slice(first, first + 128)
                col_ids = first + lax.broadcasted_iota(jnp.int32, (16, 128), 1)
                keep = (ids < my_order) & (col_ids < my_order)
                out_ref[rows, cols] = jnp.where(keep, base[rows, cols] + tile, 0.0).astype(BF16)

    for phase in range(4):
        span = mix_a.at[:, pl.ds(0, total - 1)]
        pltpu.make_async_copy(span, span, send_sem.at[phase]).wait()


def per_device(dims, vertex, bare, pp_prop, ph_prop, orders, pandya_src, pandya_sixj, back_src, back_sixj):
    m = vertex.shape[1]
    n_j, n_p = dims[:2]
    total = n_j * n_p
    band = m // total
    tiles = m // 128
    flat = vertex.reshape(m, m)
    bands = flat.reshape(total, band, tiles, 128).transpose(0, 2, 1, 3).reshape(total, tiles * band, 128)
    tile_buf = pltpu.VMEM((PARTS, total, tiles * band // PARTS, 128), BF16)
    part_buf = pltpu.VMEM((total, tiles * band // PARTS, 128), BF16)
    square = pltpu.VMEM((m, m), BF16)
    vmem = pl.BlockSpec(memory_space=pltpu.VMEM)
    hbm = pl.BlockSpec(memory_space=pltpu.HBM)
    out = pl.pallas_call(
        functools.partial(kernel, dims),
        out_shape=jax.ShapeDtypeStruct((m, m), BF16),
        in_specs=[hbm] * 10,
        out_specs=vmem,
        scratch_shapes=[
            pltpu.SMEM((total,), jnp.int32),
            pltpu.SMEM((4, total), jnp.int32),
            pltpu.SMEM((4, total), jnp.int32),
            pltpu.VMEM((1, m), F32),
            pltpu.VMEM((1, m), F32),
            pltpu.VMEM((4, band, total), F32),
            pltpu.VMEM((4, band, total), F32),
            square,
            square,
            pltpu.VMEM((m, m), F32),
            pltpu.VMEM((2, total, 4, 8, 128), F32),
            tile_buf,
            tile_buf,
            square,
            square,
            tile_buf,
            tile_buf,
            tile_buf,
            pltpu.SemaphoreType.DMA((9 + PARTS,)),
            pltpu.SemaphoreType.DMA((4,)),
            pltpu.SemaphoreType.DMA((4, PARTS)),
            pltpu.SemaphoreType.REGULAR,
        ]
        + [part_buf] * (2 * PARTS),
        compiler_params=pltpu.CompilerParams(collective_id=0, has_side_effects=True, vmem_limit_bytes=VMEM_MIB * 1024 * 1024),
        name="parquet",
    )(
        *(pltpu.with_memory_space_constraint(a, pltpu.HBM) for a in (
        orders,
        pandya_src.T,
        back_src.T,
        bands,
        flat,
        bare.reshape(m, m),
        pp_prop,
        ph_prop,
        pandya_sixj.transpose(1, 2, 0),
        back_sixj.transpose(1, 2, 0),
    )))
    return out.reshape(1, m, m)


def solution(mesh):
    n_j, n_p = mesh.shape["jown"], mesh.shape["pown"]
    cores = 2
    side = math.isqrt(n_p)
    dims = (n_j, n_p, n_j // cores, side, n_p // side, cores)
    placed = (
        P(("jown", "pown"), None, None),
        P(("jown", "pown"), None, None),
        P(("jown", "pown"), None),
        P(("jown", "pown"), None),
        P(),
        P(),
        P(None, None, ("jown", "pown")),
        P(),
        P(None, None, ("jown", "pown")),
    )
    return jax.shard_map(
        functools.partial(per_device, dims),
        mesh=mesh,
        in_specs=placed,
        out_specs=P(("jown", "pown"), None, None),
        check_vma=False,
    )
```

time: 143 us -> 114 us (0.80)
  Pallas kernels: 138 us -> 113 us
  local copies, waits for them, and re-layouts: 4.79 us -> 1.32 us
    pallas_call x1, Pallas kernels: 138 us -> 113 us  [per_device(): pl.pallas_call(functools.partial(kernel, dims), out_shape=jax.ShapeDtypeS...]
    unnamed x1, local copies, waits for them, and re-layouts: 3.08 us -> 1.32 us
    reshape x1 -> x0, local copies, waits for them, and re-layouts: 1.71 us -> none  [per_device(): pp_prop.reshape(m, 1)]
where the time goes in v2:
time: 114 us
  Pallas kernels  113 us (99%)
  local copies, waits for them, and re-layouts  1.32 us (1%)
    pallas_call x1, Pallas kernels, per_device(): pl.pallas_call(functools.partial(kernel, dims), out_shape=jax.ShapeDtypeS...  113 us

profile of v2, /device:TPU:1, one launch (start us, length us, event | category | flops | bytes accessed | tf_op | source)
XLA Modules:
  0.0 114.2 jit_solution(17693650049624616167)
XLA Ops:
  0.0 112.8 %parquet.1 = bf16[1024,1024]{1,0:T(8,128)(2,1)S(1)} custom-call(s32[128]{0:T(128)} %orders_hbm.1, s32[4,128]{1,0:T(4,128)} %bitcast.18, s32[4,128]{1,0:T(4,128)} %bitcast.19, bf16[128,64,128]{2,1,0:T(8,128)(2,1)} %bitcast.13, bf16[1024,1024]{1,0:T(8,128)(2,1)} %bitcast.14, bf16[1024,1024]{1,0:T(8,128)(2,1)} %bitcast.15, f32[1,1024]{1,0:T(1,128)} %pp_hbm.1, ...), custom_call_target="tpu_custom_call" | custom-call | tf_op jit(solution)/shard_map/parquet/pallas_call | solution.py:288
  112.9 1.3 %copy.11 = bf16[1,1024,1024]{2,1,0:T(8,128)(2,1)} copy(bf16[1,1024,1024]{2,1,0:T(8,128)(2,1)S(1)} %bitcast.12) | data formatting | bytes 4194304

commit v3 on v2

v3 whole, which is shorter than its diff:
```python
import functools
import math

import jax
import jax.numpy as jnp
from jax import lax
from jax.experimental import pallas as pl
from jax.experimental.pallas import tpu as pltpu
from jax.sharding import PartitionSpec as P

MESH = pl.DeviceIdType.MESH
F32, BF16 = jnp.float32, jnp.bfloat16
STRIDE = 37
PARTS = (4, 4)
UNROLL = 2
VMEM_MIB = 42


def kernel(
    dims,
    orders_hbm,
    psrc_hbm,
    bsrc_hbm,
    bands_hbm,
    vertex_hbm,
    bare_hbm,
    pp_hbm,
    php_hbm,
    psix_hbm,
    bsix_hbm,
    out_ref,
    orders_ref,
    psrc_ref,
    bsrc_ref,
    pp_ref,
    php_ref,
    psix_ref,
    bsix_ref,
    vbuf,
    bbuf,
    base,
    wide,
    ph,
    weighted,
    load_sem,
    send_sem,
    recv_sem,
    gate_sem,
    peers,
    *tile_bufs,
):
    n_parts = len(PARTS)
    parts = range(n_parts)
    recv_a, mix_a, ph_bands, cyc, recv_b, mix_b, ret_bands = (
        tile_bufs[n_parts * i : n_parts * (i + 1)] for i in range(7)
    )
    starts = [sum(PARTS[:part]) for part in parts]
    n_j, n_p, n_y, n_x, n_z, cores = dims
    total = n_j * n_p
    m = ph.shape[0]
    band = m // total
    me_j, me_p = lax.axis_index("jown"), lax.axis_index("pown")
    me = me_j * n_p + me_p
    my_y, my_c = me_j // cores, me_j % cores
    my_x, my_z = me_p // n_z, me_p % n_z

    owners = [[(my_y + y) % n_y * cores + (my_c + c) % cores for c in range(cores)] for y in range(n_y)]
    places = [[(my_x + x) % n_x * n_z + (my_z + z) % n_z for z in range(n_z)] for x in range(n_x)]

    def shifted(y, c, x, z):
        return owners[y][c], places[x][z]

    def offset_of(step):
        o = (step * STRIDE) % total
        z = o % n_z
        o = o // n_z
        x = o % n_x
        o = o // n_x
        return o // cores, o % cores, x, z

    def peer_of(step):
        return peers[0, step], peers[1, step], peers[2, step]

    def send(src, dst, phase, part, j, p):
        pltpu.make_async_remote_copy(
            src_ref=src,
            dst_ref=dst,
            send_sem=send_sem.at[phase, part],
            recv_sem=recv_sem.at[phase, part],
            device_id=(j, p),
            device_id_type=MESH,
        ).start()

    def wait_all(part, sem):
        span = mix_a[part].at[pl.ds(0, total - 1)]
        pltpu.make_async_copy(span, span, sem).wait()

    def arrived(phase, part):
        wait_all(part, recv_sem.at[phase, part])

    def changed(offset):
        return sum(d != 0 for d in (offset[0], offset[2], offset[3]))

    offsets = [offset_of(step) for step in range(1, total)]
    rings = [
        [o for o in offsets if changed(o) <= 1],
        [o for o in offsets if changed(o) == 2],
        [o for o in offsets if changed(o) == 3],
    ]
    along = [o for o in rings[0] if o[1] == 0]
    barrier = pltpu.get_barrier_semaphore()
    for offset in rings[0]:
        pl.semaphore_signal(barrier, inc=1, device_id=shifted(*offset), device_id_type=MESH)

    for step in range(total):
        j, p = shifted(*offset_of(step))
        peers[0, step] = j
        peers[1, step] = p
        peers[2, step] = j * n_p + p

    def load(src, dst, slot):
        copy = pltpu.make_async_copy(src, dst, load_sem.at[slot])
        copy.start()
        return copy

    rows_of = [pl.ds(starts[part] * band, PARTS[part] * band) for part in parts]
    own = [load(bands_hbm.at[me, rows_of[part]], recv_a[part].at[me], 9 + part) for part in parts]
    loads = [
        load(src, dst, slot)
        for slot, (src, dst) in enumerate(
            (
                (orders_hbm, orders_ref),
                (psrc_hbm, psrc_ref),
                (bsrc_hbm, bsrc_ref),
                (pp_hbm, pp_ref),
                (php_hbm, php_ref),
                (psix_hbm, psix_ref),
                (bsix_hbm, bsix_ref),
                (vertex_hbm, vbuf),
                (bare_hbm, bbuf),
            )
        )
    ]

    def leave_raw(part, offset):
        j, p = shifted(*offset)
        send(bands_hbm.at[j * n_p + p, rows_of[part]], recv_a[part].at[me], 0, part, j, p)

    pl.semaphore_wait(barrier, len(rings[0]))
    for stage, ring in enumerate(rings):
        if stage < 2:
            for offset in along:
                pl.semaphore_signal(gate_sem.at[stage], inc=1, device_id=shifted(*offset), device_id_type=MESH)
        for offset in ring:
            leave_raw(0, offset)
        if stage < 2:
            pl.semaphore_wait(gate_sem.at[stage], len(along))
    for part in parts[1:]:
        for offset in offsets:
            leave_raw(part, offset)

    for copy in loads:
        copy.wait()
    my_order = orders_ref[me]
    lane = lax.broadcasted_iota(jnp.int32, (8, 128), 1)
    row_id = me * band + lax.broadcasted_iota(jnp.int32, (8, 128), 0)

    def spread(six_ref, slot):
        for k in range(4):
            six = six_ref[k]
            for c in range(total):
                wide[slot, c, k] = jnp.broadcast_to(six[:, c : c + 1], (8, 128))

    spread(psix_ref, 0)

    def recouple(recv, part, mix, landing, src_ref, slot, source_mask, phase):
        first, tiles = 128 * starts[part], PARTS[part]

        def mixed(c):
            order = orders_ref[c]
            acc = [None] * tiles
            for k in range(4):
                s = src_ref[k, c]
                bound = order
                if source_mask:
                    bound = jnp.minimum(order, orders_ref[s])
                w = jnp.where(row_id < bound, wide[slot, c, k], 0.0)
                x = recv[part][s].astype(F32)
                for t in range(tiles):
                    term = w * x[8 * t : 8 * t + 8]
                    if source_mask:
                        term = jnp.where(lane < bound - (first + 128 * t), term, 0.0)
                    acc[t] = term if k == 0 else acc[t] + term
            if not source_mask:
                acc = [jnp.where(lane < order - (first + 128 * t), a, 0.0) for t, a in enumerate(acc)]
            return jnp.concatenate(acc, axis=0).astype(BF16)

        def store(step):
            c = peer_of(step)[2]
            mix[part][c] = mixed(c)

        def leave(step):
            j, p, c = peer_of(step)
            send(mix[part].at[c], landing[part].at[me], phase, part, j, p)

        store(1)

        @pl.loop(2, total, unroll=UNROLL)
        def _(step):
            store(step)
            leave(step - 1)

        landing[part][me] = mixed(me)
        leave(total - 1)

    for part in parts:
        own[part].wait()
        arrived(0, part)
        recouple(recv_a, part, mix_a, ph_bands, psrc_ref, 0, True, 1)

    col_live = (lax.broadcasted_iota(jnp.int32, (1, m), 1) < my_order).astype(F32)

    @pl.loop(0, m // 128)
    def _(i):
        rows = pl.ds(pl.multiple_of(i * 128, 128), 128)
        ids = i * 128 + lax.broadcasted_iota(jnp.int32, (128, 1), 0)
        row_live = (ids < my_order).astype(F32)
        scale = jnp.broadcast_to(pp_ref[:, rows], (128, 128)).T
        masked = vbuf[rows, :].astype(F32) * col_live * row_live
        base[rows, :] = masked
        for t in range(m // 128):
            cols = slice(128 * t, 128 * t + 128)
            weighted[rows, cols] = (masked[:, cols] * scale).astype(BF16)

    @pl.loop(0, m // 256)
    def _(i):
        rows = pl.ds(pl.multiple_of(i * 256, 256), 256)
        base[rows, :] += jnp.dot(bbuf[rows, :], weighted[...], preferred_element_type=F32)

    spread(bsix_ref, 1)

    def pair(bands, one, two):
        a = bands[one].astype(F32)
        b = bands[two].astype(F32)
        return [
            jnp.concatenate([a[8 * t : 8 * t + 8], b[8 * t : 8 * t + 8]], axis=0)
            for t in range(bands.shape[1] // 8)
        ]

    for part in parts:
        arrived(1, part)

        @pl.loop(0, total // 2, unroll=UNROLL)
        def _(q):
            rows = pl.ds(pl.multiple_of(q * 16, 16), 16)
            for t, tile in enumerate(pair(ph_bands[part], 2 * q, 2 * q + 1)):
                ph[rows, 128 * (starts[part] + t) : 128 * (starts[part] + t) + 128] = tile.astype(BF16)
            for t, tile in enumerate(pair(ph_bands[part], peer_of(2 * q)[2], peer_of(2 * q + 1)[2])):
                cols = slice(128 * (starts[part] + t), 128 * (starts[part] + t) + 128)
                weighted[rows, cols] = (tile * php_ref[:, cols]).astype(BF16)

    per_chunk = 256 // band
    for part in parts:
        cols = slice(128 * starts[part], 128 * (starts[part] + PARTS[part]))

        @pl.loop(0, total // per_chunk)
        def _(i):
            rows = pl.ds(pl.multiple_of(i * 256, 256), 256)
            prod = jnp.dot(weighted[rows, :], ph[:, cols], preferred_element_type=F32)
            prod = prod * (1.0 / math.sqrt(m))
            for b in range(per_chunk):
                lines = [prod[band * b : band * b + band, 128 * t : 128 * t + 128] for t in range(PARTS[part])]
                cyc[part][i * per_chunk + b] = jnp.concatenate(lines, axis=0).astype(BF16)

            @pl.loop(0, per_chunk)
            def _(b):
                step = i * per_chunk + b

                @pl.when(step > 0)
                def _():
                    j, p, _ = peer_of(step)
                    send(cyc[part].at[step], recv_b[part].at[me], 2, part, j, p)

        recv_b[part][me] = cyc[part][0]

    for part in parts:
        arrived(2, part)
        recouple(recv_b, part, mix_b, ret_bands, bsrc_ref, 1, False, 3)

    for part in parts:
        arrived(3, part)

        @pl.loop(0, total // 2, unroll=UNROLL)
        def _(q):
            rows = pl.ds(pl.multiple_of(q * 16, 16), 16)
            ids = q * 16 + lax.broadcasted_iota(jnp.int32, (16, 128), 0)
            for t, tile in enumerate(pair(ret_bands[part], 2 * q, 2 * q + 1)):
                first = 128 * (starts[part] + t)
                cols = slice(first, first + 128)
                col_ids = first + lax.broadcasted_iota(jnp.int32, (16, 128), 1)
                keep = (ids < my_order) & (col_ids < my_order)
                out_ref[rows, cols] = jnp.where(keep, base[rows, cols] + tile, 0.0).astype(BF16)

    for phase in range(4):
        for part in parts:
            wait_all(part, send_sem.at[phase, part])


def per_device(dims, vertex, bare, pp_prop, ph_prop, orders, pandya_src, pandya_sixj, back_src, back_sixj):
    m = vertex.shape[1]
    n_j, n_p = dims[:2]
    total = n_j * n_p
    band = m // total
    tiles = m // 128
    flat = vertex.reshape(m, m)
    bands = flat.reshape(total, band, tiles, 128).transpose(0, 2, 1, 3).reshape(total, tiles * band, 128)
    part_bufs = [pltpu.VMEM((total, band * part, 128), BF16) for part in PARTS]
    square = pltpu.VMEM((m, m), BF16)
    vmem = pl.BlockSpec(memory_space=pltpu.VMEM)
    hbm = pl.BlockSpec(memory_space=pltpu.HBM)
    out = pl.pallas_call(
        functools.partial(kernel, dims),
        out_shape=jax.ShapeDtypeStruct((m, m), BF16),
        in_specs=[hbm] * 10,
        out_specs=vmem,
        scratch_shapes=[
            pltpu.SMEM((total,), jnp.int32),
            pltpu.SMEM((4, total), jnp.int32),
            pltpu.SMEM((4, total), jnp.int32),
            pltpu.VMEM((1, m), F32),
            pltpu.VMEM((1, m), F32),
            pltpu.VMEM((4, band, total), F32),
            pltpu.VMEM((4, band, total), F32),
            square,
            square,
            pltpu.VMEM((m, m), F32),
            pltpu.VMEM((2, total, 4, 8, 128), F32),
            square,
            square,
            pltpu.SemaphoreType.DMA((9 + len(PARTS),)),
            pltpu.SemaphoreType.DMA((4, len(PARTS))),
            pltpu.SemaphoreType.DMA((4, len(PARTS))),
            pltpu.SemaphoreType.REGULAR((2,)),
            pltpu.SMEM((3, total), jnp.int32),
        ]
        + part_bufs * 7,
        compiler_params=pltpu.CompilerParams(collective_id=0, has_side_effects=True, vmem_limit_bytes=VMEM_MIB * 1024 * 1024),
        name="parquet",
    )(
        *(pltpu.with_memory_space_constraint(a, pltpu.HBM) for a in (
        orders,
        pandya_src.T,
        back_src.T,
        bands,
        flat,
        bare.reshape(m, m),
        pp_prop,
        ph_prop,
        pandya_sixj.transpose(1, 2, 0),
        back_sixj.transpose(1, 2, 0),
    )))
    return out.reshape(1, m, m)


def solution(mesh):
    n_j, n_p = mesh.shape["jown"], mesh.shape["pown"]
    cores = 2
    side = math.isqrt(n_p)
    dims = (n_j, n_p, n_j // cores, side, n_p // side, cores)
    placed = (
        P(("jown", "pown"), None, None),
        P(("jown", "pown"), None, None),
        P(("jown", "pown"), None),
        P(("jown", "pown"), None),
        P(),
        P(),
        P(None, None, ("jown", "pown")),
        P(),
        P(None, None, ("jown", "pown")),
    )
    return jax.shard_map(
        functools.partial(per_device, dims),
        mesh=mesh,
        in_specs=placed,
        out_specs=P(("jown", "pown"), None, None),
        check_vma=False,
    )
```

time: 114 us -> 111 us (0.974)
  Pallas kernels: 113 us -> 110 us
    pallas_call x1, Pallas kernels: 113 us -> 110 us  [per_device(): pl.pallas_call(functools.partial(kernel, dims), out_shape=jax.ShapeDtypeS...]
where the time goes in v3:
time: 111 us
  Pallas kernels  110 us (99%)
  local copies, waits for them, and re-layouts  1.32 us (1%)
    pallas_call x1, Pallas kernels, per_device(): pl.pallas_call(functools.partial(kernel, dims), out_shape=jax.ShapeDtypeS...  110 us

profile of v3, /device:TPU:1, one launch (start us, length us, event | category | flops | bytes accessed | tf_op | source)
XLA Modules:
  0.0 111.0 jit_solution(14693357436487156858)
XLA Ops:
  0.0 109.7 %parquet.1 = bf16[1024,1024]{1,0:T(8,128)(2,1)S(1)} custom-call(s32[128]{0:T(128)} %orders_hbm.1, s32[4,128]{1,0:T(4,128)} %bitcast.18, s32[4,128]{1,0:T(4,128)} %bitcast.19, bf16[128,64,128]{2,1,0:T(8,128)(2,1)} %bitcast.13, bf16[1024,1024]{1,0:T(8,128)(2,1)} %bitcast.14, bf16[1024,1024]{1,0:T(8,128)(2,1)} %bitcast.15, f32[1,1024]{1,0:T(1,128)} %pp_hbm.1, ...), custom_call_target="tpu_custom_call" | custom-call | tf_op jit(solution)/shard_map/parquet/pallas_call | solution.py:321
  109.7 1.3 %copy.11 = bf16[1,1024,1024]{2,1,0:T(8,128)(2,1)} copy(bf16[1,1024,1024]{2,1,0:T(8,128)(2,1)S(1)} %bitcast.12) | data formatting | bytes 4194304

commit v4 on v3

--- a/solution.py
+++ b/solution.py
@@ -11,9 +11,10 @@
 MESH = pl.DeviceIdType.MESH
 F32, BF16 = jnp.float32, jnp.bfloat16
 STRIDE = 37
-PARTS = (4, 4)
-UNROLL = 2
-VMEM_MIB = 42
+PARTS = (6, 2)
+UNROLL = 4
+CHUNK = 256
+VMEM_MIB = 44
 
 
 def kernel(
@@ -47,6 +48,7 @@
     recv_sem,
     gate_sem,
     peers,
+    early,
     *tile_bufs,
 ):
     n_parts = len(PARTS)
@@ -111,12 +113,6 @@
     barrier = pltpu.get_barrier_semaphore()
     for offset in rings[0]:
         pl.semaphore_signal(barrier, inc=1, device_id=shifted(*offset), device_id_type=MESH)
-
-    for step in range(total):
-        j, p = shifted(*offset_of(step))
-        peers[0, step] = j
-        peers[1, step] = p
-        peers[2, step] = j * n_p + p
 
     def load(src, dst, slot):
         copy = pltpu.make_async_copy(src, dst, load_sem.at[slot])
@@ -159,6 +155,12 @@
         for offset in offsets:
             leave_raw(part, offset)
 
+    for step in range(total):
+        j, p = shifted(*offset_of(step))
+        peers[0, step] = j
+        peers[1, step] = p
+        peers[2, step] = j * n_p + p
+
     for copy in loads:
         copy.wait()
     my_order = orders_ref[me]
@@ -247,40 +249,69 @@
             for t in range(bands.shape[1] // 8)
         ]
 
-    for part in parts:
-        arrived(1, part)
-
+    def columns(part):
+        return slice(128 * starts[part], 128 * (starts[part] + PARTS[part]))
+
+    def place_ph(part):
         @pl.loop(0, total // 2, unroll=UNROLL)
         def _(q):
             rows = pl.ds(pl.multiple_of(q * 16, 16), 16)
             for t, tile in enumerate(pair(ph_bands[part], 2 * q, 2 * q + 1)):
                 ph[rows, 128 * (starts[part] + t) : 128 * (starts[part] + t) + 128] = tile.astype(BF16)
+
+    def place_weighted(part, first, count):
+        @pl.loop(0, count, unroll=UNROLL)
+        def _(at):
+            q = first + at
+            rows = pl.ds(pl.multiple_of(q * 16, 16), 16)
             for t, tile in enumerate(pair(ph_bands[part], peer_of(2 * q)[2], peer_of(2 * q + 1)[2])):
                 cols = slice(128 * (starts[part] + t), 128 * (starts[part] + t) + 128)
                 weighted[rows, cols] = (tile * php_ref[:, cols]).astype(BF16)
 
-    per_chunk = 256 // band
+    per_chunk = CHUNK // band
+
+    def leave_product(part, i, prod):
+        prod = prod * (1.0 / math.sqrt(m))
+        for b in range(per_chunk):
+            lines = [prod[band * b : band * b + band, 128 * t : 128 * t + 128] for t in range(PARTS[part])]
+            cyc[part][i * per_chunk + b] = jnp.concatenate(lines, axis=0).astype(BF16)
+
+        @pl.loop(0, per_chunk)
+        def _(b):
+            step = i * per_chunk + b
+
+            @pl.when(step > 0)
+            def _():
+                j, p, _ = peer_of(step)
+                send(cyc[part].at[step], recv_b[part].at[me], 2, part, j, p)
+
+    left, right = columns(0), columns(1)
+    arrived(1, 0)
+    place_ph(0)
+    place_weighted(0, 0, total // 2)
+
+    @pl.loop(0, m // CHUNK)
+    def _(i):
+        rows = pl.ds(pl.multiple_of(i * CHUNK, CHUNK), CHUNK)
+        early[rows, :] = jnp.dot(weighted[rows, left], ph[left, left], preferred_element_type=F32)
+
+    arrived(1, 1)
+
+    @pl.loop(0, m // CHUNK)
+    def _(i):
+        rows = pl.ds(pl.multiple_of(i * CHUNK, CHUNK), CHUNK)
+        place_weighted(1, i * (per_chunk // 2), per_chunk // 2)
+        late = jnp.dot(weighted[rows, right], ph[right, left], preferred_element_type=F32)
+        leave_product(0, i, early[rows, :] + late)
+
+    place_ph(1)
+
+    @pl.loop(0, m // CHUNK)
+    def _(i):
+        rows = pl.ds(pl.multiple_of(i * CHUNK, CHUNK), CHUNK)
+        leave_product(1, i, jnp.dot(weighted[rows, :], ph[:, right], preferred_element_type=F32))
+
     for part in parts:
-        cols = slice(128 * starts[part], 128 * (starts[part] + PARTS[part]))
-
-        @pl.loop(0, total // per_chunk)
-        def _(i):
-            rows = pl.ds(pl.multiple_of(i * 256, 256), 256)
-            prod = jnp.dot(weighted[rows, :], ph[:, cols], preferred_element_type=F32)
-            prod = prod * (1.0 / math.sqrt(m))
-            for b in range(per_chunk):
-                lines = [prod[band * b : band * b + band, 128 * t : 128 * t + 128] for t in range(PARTS[part])]
-                cyc[part][i * per_chunk + b] = jnp.concatenate(lines, axis=0).astype(BF16)
-
-            @pl.loop(0, per_chunk)
-            def _(b):
-                step = i * per_chunk + b
-
-                @pl.when(step > 0)
-                def _():
-                    j, p, _ = peer_of(step)
-                    send(cyc[part].at[step], recv_b[part].at[me], 2, part, j, p)
-
         recv_b[part][me] = cyc[part][0]
 
     for part in parts:
@@ -342,6 +373,7 @@
             pltpu.SemaphoreType.DMA((4, len(PARTS))),
             pltpu.SemaphoreType.REGULAR((2,)),
             pltpu.SMEM((3, total), jnp.int32),
+            pltpu.VMEM((m, 128 * PARTS[0]), F32),
         ]
         + part_bufs * 7,
         compiler_params=pltpu.CompilerParams(collective_id=0, has_side_effects=True, vmem_limit_bytes=VMEM_MIB * 1024 * 1024),

time: 111 us -> 110 us (level)
  Pallas kernels: 110 us -> 108 us
    pallas_call x1, Pallas kernels: 110 us -> 108 us  [per_device(): pl.pallas_call(functools.partial(kernel, dims), out_shape=jax.ShapeDtypeS...]
where the time goes in v4:
time: 110 us; the launch traced here: 109 us
  Pallas kernels  108 us (98%)
  local copies, waits for them, and re-layouts  1.32 us (1%)
    pallas_call x1, Pallas kernels, per_device(): pl.pallas_call(functools.partial(kernel, dims), out_shape=jax.ShapeDtypeS...  108 us

profile of v4, /device:TPU:1, one launch (start us, length us, event | category | flops | bytes accessed | tf_op | source)
XLA Modules:
  0.0 109.4 jit_solution(6704131034041450628)
XLA Ops:
  0.0 108.1 %parquet.1 = bf16[1024,1024]{1,0:T(8,128)(2,1)S(1)} custom-call(s32[128]{0:T(128)} %orders_hbm.1, s32[4,128]{1,0:T(4,128)} %bitcast.18, s32[4,128]{1,0:T(4,128)} %bitcast.19, bf16[128,64,128]{2,1,0:T(8,128)(2,1)} %bitcast.13, bf16[1024,1024]{1,0:T(8,128)(2,1)} %bitcast.14, bf16[1024,1024]{1,0:T(8,128)(2,1)} %bitcast.15, f32[1,1024]{1,0:T(1,128)} %pp_hbm.1, ...), custom_call_target="tpu_custom_call" | custom-call | tf_op jit(solution)/shard_map/parquet/pallas_call | solution.py:352
  108.1 1.3 %copy.11 = bf16[1,1024,1024]{2,1,0:T(8,128)(2,1)} copy(bf16[1,1024,1024]{2,1,0:T(8,128)(2,1)S(1)} %bitcast.12) | data formatting | bytes 4194304

commit v5 on v4

--- a/solution.py
+++ b/solution.py
@@ -10,11 +10,11 @@
 
 MESH = pl.DeviceIdType.MESH
 F32, BF16 = jnp.float32, jnp.bfloat16
-STRIDE = 37
+STRIDE = 45
 PARTS = (6, 2)
 UNROLL = 4
 CHUNK = 256
-VMEM_MIB = 44
+VMEM_MIB = 47
 
 
 def kernel(
@@ -49,6 +49,7 @@
     gate_sem,
     peers,
     early,
+    bands,
     *tile_bufs,
 ):
     n_parts = len(PARTS)
@@ -119,6 +120,7 @@
         copy.start()
         return copy
 
+    raw = load(bands_hbm, bands, 9 + n_parts)
     rows_of = [pl.ds(starts[part] * band, PARTS[part] * band) for part in parts]
     own = [load(bands_hbm.at[me, rows_of[part]], recv_a[part].at[me], 9 + part) for part in parts]
     loads = [
@@ -140,20 +142,23 @@
 
     def leave_raw(part, offset):
         j, p = shifted(*offset)
-        send(bands_hbm.at[j * n_p + p, rows_of[part]], recv_a[part].at[me], 0, part, j, p)
+        send(bands.at[j * n_p + p, rows_of[part]], recv_a[part].at[me], 0, part, j, p)
 
     pl.semaphore_wait(barrier, len(rings[0]))
+    raw.wait()
     for stage, ring in enumerate(rings):
         if stage < 2:
             for offset in along:
                 pl.semaphore_signal(gate_sem.at[stage], inc=1, device_id=shifted(*offset), device_id_type=MESH)
-        for offset in ring:
-            leave_raw(0, offset)
+        for part in parts if stage == 0 else (0,):
+            for offset in ring:
+                leave_raw(part, offset)
         if stage < 2:
             pl.semaphore_wait(gate_sem.at[stage], len(along))
     for part in parts[1:]:
         for offset in offsets:
-            leave_raw(part, offset)
+            if offset not in rings[0]:
+                leave_raw(part, offset)
 
     for step in range(total):
         j, p = shifted(*offset_of(step))
@@ -368,12 +373,13 @@
             pltpu.VMEM((2, total, 4, 8, 128), F32),
             square,
             square,
-            pltpu.SemaphoreType.DMA((9 + len(PARTS),)),
+            pltpu.SemaphoreType.DMA((10 + len(PARTS),)),
             pltpu.SemaphoreType.DMA((4, len(PARTS))),
             pltpu.SemaphoreType.DMA((4, len(PARTS))),
             pltpu.SemaphoreType.REGULAR((2,)),
             pltpu.SMEM((3, total), jnp.int32),
             pltpu.VMEM((m, 128 * PARTS[0]), F32),
+            pltpu.VMEM((total, m * band // 128, 128), BF16),
         ]
         + part_bufs * 7,
         compiler_params=pltpu.CompilerParams(collective_id=0, has_side_effects=True, vmem_limit_bytes=VMEM_MIB * 1024 * 1024),

time: 110 us -> 109 us (level)
  no operation moved by 1% of the time
where the time goes in v5:
time: 109 us
  Pallas kernels  108 us (99%)
  local copies, waits for them, and re-layouts  1.32 us (1%)
    pallas_call x1, Pallas kernels, per_device(): pl.pallas_call(functools.partial(kernel, dims), out_shape=jax.ShapeDtypeS...  108 us

profile of v5, /device:TPU:1, one launch (start us, length us, event | category | flops | bytes accessed | tf_op | source)
XLA Modules:
  0.0 109.1 jit_solution(15016511774134384843)
XLA Ops:
  0.0 107.7 %parquet.1 = bf16[1024,1024]{1,0:T(8,128)(2,1)S(1)} custom-call(s32[128]{0:T(128)} %orders_hbm.1, s32[4,128]{1,0:T(4,128)} %bitcast.18, s32[4,128]{1,0:T(4,128)} %bitcast.19, bf16[128,64,128]{2,1,0:T(8,128)(2,1)} %bitcast.13, bf16[1024,1024]{1,0:T(8,128)(2,1)} %bitcast.14, bf16[1024,1024]{1,0:T(8,128)(2,1)} %bitcast.15, f32[1,1024]{1,0:T(1,128)} %pp_hbm.1, ...), custom_call_target="tpu_custom_call" | custom-call | tf_op jit(solution)/shard_map/parquet/pallas_call | solution.py:357
  107.7 1.3 %copy.11 = bf16[1,1024,1024]{2,1,0:T(8,128)(2,1)} copy(bf16[1,1024,1024]{2,1,0:T(8,128)(2,1)S(1)} %bitcast.12) | data formatting | bytes 4194304
